TPU v7x, 32 devices: a whole 2x2x4 slice. The times are simulated.
32 devices in a mesh: gx: 8 (over y, x, core), gy: 4 (over z).
Axes of the slice: x: 2, y: 2, z: 4, core: 2. Of those that a mesh axis runs over, the one named last changes fastest.
Arguments:
- obstacles: int32 [1024, 1024], P('gx', 'gy'), may hold values 0 or 1
- load: float32 [1024, 1024], P('gx', 'gy'), may hold values from 0.25 to 4
- exit_rows: int32 [4, 256], replicated, may hold values from 0 to 1023
- exit_cols: int32 [4, 256], replicated, may hold values from 0 to 1023
Outputs:
- potential: float32 [4, 1024, 1024], P(None, 'gx', 'gy')
All inputs are finite; a program needn't handle non-finite values. No bound on the sum of `obstacles` on one device may be relied on, other than what follows from the above.
Results may differ from a plain program's by a relative error of at most 0.0001.
Values sent between devices are 32-bit elements; how exact they have to be, the bound alone decides.
A program may use at most 64 MiB of HBM per device.

v0:
```python
import jax
import jax.numpy as jnp
from jax import lax
from jax.sharding import PartitionSpec as P

COARSEN = 4
SMOOTH = 4
CSWEEPS = 4


SCREENING = 0.0001
EXIT_SINK = 4.0
COARSE_SHIFT = 0.01
DAMPING = 0.8
UPPER_BOUND = 12.5
LOWER_BOUND = 1.0


def with_halo(x, sides, width):
    for axis, dim in sides:
        peers, length = (lax.axis_size(axis), x.shape[dim])
        up = [(i, (i + 1) % peers) for i in range(peers - 1)]
        down = [(j, i) for i, j in up]
        last = lax.slice_in_dim(x, length - width, length, axis=dim)
        initial = lax.slice_in_dim(x, 0, width, axis=dim)
        before = lax.ppermute(last, axis, up)
        after = lax.ppermute(initial, axis, down)
        x = jnp.concatenate([before, x, after], axis=dim)
    return x


def cross_inner(padded):
    return padded[:, 2:, 1:-1] + padded[:, :-2, 1:-1] + padded[:, 1:-1, 2:] + padded[:, 1:-1, :-2]


def cross_local(field):
    return cross_inner(jnp.pad(field, ((0, 0), (1, 1), (1, 1))))


def chebyshev(start, residual, operate):
    center = 0.5 * (UPPER_BOUND + LOWER_BOUND)
    half_span = 0.5 * (UPPER_BOUND - LOWER_BOUND)
    sigma_ratio = center / half_span
    ratio_old = 1.0 / sigma_ratio
    update = residual / center
    result = start + update
    for sweep in range(SMOOTH - 1):
        residual = residual - operate(update)
        ratio_new = 1.0 / (2.0 * sigma_ratio - ratio_old)
        update = ratio_new * ratio_old * update + 2.0 * ratio_new / half_span * residual
        result = result + update
        ratio_old = ratio_new
    return result


def restrict(residual):
    goals, height, width = residual.shape
    blocks = residual.reshape(goals, height // COARSEN, COARSEN, width // COARSEN, COARSEN)
    return blocks.mean(axis=(2, 4))


def prolong(estimate, open_cells):
    expanded = jnp.repeat(jnp.repeat(estimate, COARSEN, axis=1), COARSEN, axis=2)
    return open_cells * expanded


def column_mask(width, reach):
    column = lax.axis_index("gy") * width + jnp.arange(width + 2 * reach, dtype=jnp.int32) - reach
    return ((column >= 0) & (column < lax.axis_size("gy") * width)).astype(jnp.float32)[
        None, None, :
    ]


def coarse_solve(coarse_rhs):
    center_weight = 4.0 + COARSE_SHIFT
    reach = CSWEEPS - 1
    width = coarse_rhs.shape[2]
    widened = with_halo(coarse_rhs, (("gy", 2),), reach)
    col_mask = column_mask(width, reach)
    estimate = DAMPING * widened / center_weight * col_mask
    for sweep in range(CSWEEPS - 1):
        padded = with_halo(estimate, (("gx", 1),), 1)
        padded = jnp.pad(padded, ((0, 0), (0, 0), (1, 1)))
        estimate = (
            estimate
            + DAMPING * (widened - (center_weight * estimate - cross_inner(padded))) / center_weight
        ) * col_mask
    return estimate[:, :, reach : reach + width]


def per_device(obstacles, load, exit_rows, exit_cols):
    tile_rows, tile_cols = obstacles.shape
    goals = exit_rows.shape[0]
    open_int = 1 - obstacles
    margin = SMOOTH - 1
    walls = with_halo(open_int, (("gx", 0), ("gy", 1)), margin + 1).astype(jnp.float32)
    wide_rows = tile_rows + 2 * margin
    wide_cols = tile_cols + 2 * margin
    open_wide = walls[1:-1, 1:-1]
    neighbours = walls[2:, 1:-1] + walls[:-2, 1:-1] + walls[1:-1, 2:] + walls[1:-1, :-2]
    local_rows = exit_rows - lax.axis_index("gx") * tile_rows + margin
    local_cols = exit_cols - lax.axis_index("gy") * tile_cols + margin
    inside = (
        (local_rows >= 0) & (local_rows < wide_rows) & (local_cols >= 0) & (local_cols < wide_cols)
    )
    flat_index = jnp.where(inside, local_rows * wide_cols + local_cols, wide_rows * wide_cols)
    goal_index = jnp.broadcast_to(jnp.arange(goals, dtype=jnp.int32)[:, None], flat_index.shape)
    marks = (
        jnp.zeros((goals, wide_rows * wide_cols), jnp.float32)
        .at[goal_index, flat_index]
        .add(1.0, mode="drop")
    )
    exits = jnp.minimum(marks, 1.0).reshape(goals, wide_rows, wide_cols)
    diag_wide = (
        SCREENING + 4.0 * (1.0 - open_wide) + open_wide * neighbours + EXIT_SINK * open_wide * exits
    )
    open_cells = open_wide[margin : margin + tile_rows, margin : margin + tile_cols]
    diagonal = diag_wide[:, margin : margin + tile_rows, margin : margin + tile_cols]

    def operate_wide(field):
        return diag_wide * field - open_wide * cross_local(open_wide * field)

    def smooth(start, residual):
        extended = with_halo(residual, (("gx", 1), ("gy", 2)), margin)
        start_wide = jnp.pad(start, ((0, 0), (margin, margin), (margin, margin)))
        result = chebyshev(start_wide, extended, operate_wide)
        return result[:, margin : margin + tile_rows, margin : margin + tile_cols]

    source = jnp.broadcast_to(open_cells * load, (goals, tile_rows, tile_cols))
    potential = smooth(jnp.zeros_like(source), source)
    estimate = coarse_solve(restrict(source))
    correction = prolong(estimate, open_cells)
    padded_pair = (
        with_halo(open_cells * potential, (("gx", 1), ("gy", 2)), 1),
        with_halo(open_cells * correction, (("gx", 1), ("gy", 2)), 1),
    )
    residual = source - (diagonal * potential - open_cells * cross_inner(padded_pair[0]))
    shifted = residual - (diagonal * correction - open_cells * cross_inner(padded_pair[1]))
    estimate_next = coarse_solve(restrict(residual))
    potential = smooth(potential + correction, shifted)
    return potential + prolong(estimate_next, open_cells)


def solution(mesh):
    in_specs = (P("gx", "gy"), P("gx", "gy"), P(), P())
    out_specs = P(None, "gx", "gy")
    return jax.shard_map(
        per_device, mesh=mesh, in_specs=in_specs, out_specs=out_specs, check_vma=False
    )
```

profile of v0, /device:TPU:3, one launch (start us, length us, event | category | flops | bytes accessed | tf_op | source)
XLA Modules:
  0.0 210.3 jit_solution(7291258563090103888)
XLA Ops:
  0.0 0.9 broadcast_subtract_fusion
  0.9 3.7 %collective-permute-start = (s32[4,256]{1,0:T(4,128)S(1)}, s32[4,256]{1,0:T(4,128)S(1)}, u32[]{:S(2)}, u32[]{:S(2)}) collective-permute-start(s32[4,256]{1,0:T(4,128)S(1)} %get-tuple-element.55), channel_id=1, source_target_pairs={{0,4},{4,8},{8,12},{12,16},{16,20},{20,24},{24,28},{1,5},{5,9},{9,... | collective-permute-start | bytes 12296 | tf_op jit(solution)/shard_map/ppermute | solution.py:26
  4.6 1.9 collective-permute-start.1
  8.8 6.0 %scatter_custom_fusion = f32[140432]{0:T(1024)S(1)} fusion(s32[1024]{0:T(1024)S(1)} %bitcast.13, f32[1024]{0:T(1024)S(1)} %broadcast.192, f32[]{:T(128)} %constant.29.clone.1), kind=kCustom, calls=%fused_computation.76 | custom fusion | flops 1024 | bytes 561732
  15.0 3.2 %collective-permute-start.2 = (s32[136,4]{1,0:T(8,128)S(1)}, s32[136,4]{1,0:T(8,128)S(1)}, u32[]{:S(2)}, u32[]{:S(2)}) collective-permute-start(s32[136,4]{1,0:T(8,128)S(1)} %get-tuple-element.51), channel_id=1, source_target_pairs={{0,1},{1,2},{2,3},{4,5},{5,6},{6,7},{8,9},{9,10},{10,11},{12,13},{... | collective-permute-start | bytes 6536 | tf_op jit(solution)/shard_map/ppermute | solution.py:26
  18.2 1.3 collective-permute-start.3
  19.6 3.7 %collective-permute-done.3 = s32[136,4]{1,0:T(8,128)S(1)} collective-permute-done((s32[136,4]{1,0:T(8,128)S(1)}, s32[136,4]{1,0:T(8,128)S(1)}, u32[]{:S(2)}, u32[]{:S(2)}) %collective-permute-start.3) | collective-permute-done | bytes 2208 | tf_op jit(solution)/shard_map/ppermute | solution.py:27
  23.4 1.0 fusion.73
  24.4 5.7 %broadcast_in_dim.75 = f32[32,4,64,4]{3,2,1,0:T(8,128)} reshape(f32[128,256]{1,0:T(8,128)S(1)} %get-tuple-element.50) | data formatting | bytes 262144 | tf_op jit(solution)/shard_map/broadcast_in_dim | solution.py:129
  30.2 2.5 %reduce_sum.24 = f32[32,64]{1,0:T(8,128)S(1)} reduce(f32[32,4,64,4]{3,2,1,0:T(8,128)} %broadcast_in_dim.75, f32[]{:T(128)} %constant.29.clone.1), dimensions={1,3}, to_apply=%region_1.2 | reduce | flops 30720 | bytes 139268 | tf_op jit(solution)/shard_map/reduce_sum | solution.py:59
  32.8 3.2 %collective-permute-start.8 = (f32[4,32,3]{2,1,0:T(8,128)S(1)}, f32[4,32,3]{2,1,0:T(8,128)S(1)}, u32[]{:S(2)}, u32[]{:S(2)}) collective-permute-start(f32[4,32,3]{2,1,0:T(8,128)S(1)} %reduce_sum.25), channel_id=1, source_target_pairs={{0,1},{1,2},{2,3},{4,5},{5,6},{6,7},{8,9},{9,10},{10,11},{12,13},{... | collective-permute-start | bytes 4616 | tf_op jit(solution)/shard_map/ppermute | solution.py:26
  36.0 1.3 collective-permute-start.9
  37.4 3.7 %collective-permute-done.9 = f32[4,32,3]{2,1,0:T(8,128)S(1)} collective-permute-done((f32[4,32,3]{2,1,0:T(8,128)S(1)}, f32[4,32,3]{2,1,0:T(8,128)S(1)}, u32[]{:S(2)}, u32[]{:S(2)}) %collective-permute-start.9) | collective-permute-done | bytes 1568 | tf_op jit(solution)/shard_map/ppermute | solution.py:27
  41.2 5.4 %collective-permute-start.10 = (f32[4,1,70]{2,1,0:T(1,128)S(1)}, f32[4,1,70]{2,1,0:T(1,128)S(1)}, u32[]{:S(2)}, u32[]{:S(2)}) collective-permute-start(f32[4,1,70]{2,1,0:T(1,128)S(1)} %get-tuple-element.74), channel_id=1, source_target_pairs={{4,0},{8,4},{12,8},{16,12},{20,16},{24,20},{28,24},{5,1},{9,5},{13... | collective-permute-start | bytes 3368 | tf_op jit(solution)/shard_map/ppermute | solution.py:27
  46.6 3.9 %collective-permute-start.11 = (f32[4,1,70]{2,1,0:T(1,128)S(1)}, f32[4,1,70]{2,1,0:T(1,128)S(1)}, u32[]{:S(2)}, u32[]{:S(2)}) collective-permute-start(f32[4,1,70]{2,1,0:T(1,128)S(1)} %get-tuple-element.73), channel_id=1, source_target_pairs={{0,4},{4,8},{8,12},{12,16},{16,20},{20,24},{24,28},{1,5},{5,9},{9,... | collective-permute-start | bytes 3368 | tf_op jit(solution)/shard_map/ppermute | solution.py:26
  51.4 2.2 %collective-permute-start.12 = (f32[4,1,70]{2,1,0:T(1,128)S(1)}, f32[4,1,70]{2,1,0:T(1,128)S(1)}, u32[]{:S(2)}, u32[]{:S(2)}) collective-permute-start(f32[4,1,70]{2,1,0:T(1,128)S(1)} %get-tuple-element.72), channel_id=1, source_target_pairs={{4,0},{8,4},{12,8},{16,12},{20,16},{24,20},{28,24},{5,1},{9,5},{13... | collective-permute-start | bytes 3368 | tf_op jit(solution)/shard_map/ppermute | solution.py:27
  53.6 4.8 %collective-permute-start.13 = (f32[4,1,70]{2,1,0:T(1,128)S(1)}, f32[4,1,70]{2,1,0:T(1,128)S(1)}, u32[]{:S(2)}, u32[]{:S(2)}) collective-permute-start(f32[4,1,70]{2,1,0:T(1,128)S(1)} %get-tuple-element.71), channel_id=1, source_target_pairs={{0,4},{4,8},{8,12},{12,16},{16,20},{20,24},{24,28},{1,5},{5,9},{9,... | collective-permute-start | bytes 3368 | tf_op jit(solution)/shard_map/ppermute | solution.py:26
  58.5 1.1 fusion.26
  59.8 1.9 collective-permute-start.14
  61.7 4.7 %collective-permute-start.15 = (f32[4,1,70]{2,1,0:T(1,128)S(1)}, f32[4,1,70]{2,1,0:T(1,128)S(1)}, u32[]{:S(2)}, u32[]{:S(2)}) collective-permute-start(f32[4,1,70]{2,1,0:T(1,128)S(1)} %get-tuple-element.69), channel_id=1, source_target_pairs={{0,4},{4,8},{8,12},{12,16},{16,20},{20,24},{24,28},{1,5},{5,9},{9,... | collective-permute-start | bytes 3368 | tf_op jit(solution)/shard_map/ppermute | solution.py:26
  66.4 2.4 %collective-permute-start.4 = (f32[4,3,256]{2,1,0:T(4,128)S(1)}, f32[4,3,256]{2,1,0:T(4,128)S(1)}, u32[]{:S(2)}, u32[]{:S(2)}) collective-permute-start(f32[4,3,256]{2,1,0:T(4,128)S(1)} %broadcast_in_dim.31), channel_id=1, source_target_pairs={{0,4},{4,8},{8,12},{12,16},{16,20},{20,24},{24,28},{1,5},{5,9},{9,... | collective-permute-start | bytes 36872 | tf_op jit(solution)/shard_map/ppermute | solution.py:26
  68.9 1.9 collective-permute-start.5
  71.0 3.8 %collective-permute-done.5 = f32[4,3,256]{2,1,0:T(4,128)S(1)} collective-permute-done((f32[4,3,256]{2,1,0:T(4,128)S(1)}, f32[4,3,256]{2,1,0:T(4,128)S(1)}, u32[]{:S(2)}, u32[]{:S(2)}) %collective-permute-start.5) | collective-permute-done | bytes 12320 | tf_op jit(solution)/shard_map/ppermute | solution.py:27
  74.9 0.9 fusion.68
  75.8 3.2 %collective-permute-start.6 = (f32[4,134,3]{2,1,0:T(8,128)}, f32[4,134,3]{2,1,0:T(8,128)S(1)}, u32[]{:S(2)}, u32[]{:S(2)}) collective-permute-start(f32[4,134,3]{2,1,0:T(8,128)} %get-tuple-element.35), channel_id=1, source_target_pairs={{0,1},{1,2},{2,3},{4,5},{5,6},{6,7},{8,9},{9,10},{10,11},{12,13},{... | collective-permute-start | bytes 19304 | tf_op jit(solution)/shard_map/ppermute | solution.py:26
  79.1 1.3 collective-permute-start.7
  81.0 2.7 %collective-permute-done.6 = f32[4,134,3]{2,1,0:T(8,128)S(1)} collective-permute-done((f32[4,134,3]{2,1,0:T(8,128)}, f32[4,134,3]{2,1,0:T(8,128)S(1)}, u32[]{:S(2)}, u32[]{:S(2)}) %collective-permute-start.6) | collective-permute-done | bytes 6464 | tf_op jit(solution)/shard_map/ppermute | solution.py:26
  83.7 4.1 %collective-permute-done.7 = f32[4,134,3]{2,1,0:T(8,128)} collective-permute-done((f32[4,134,3]{2,1,0:T(8,128)}, f32[4,134,3]{2,1,0:T(8,128)}, u32[]{:S(2)}, u32[]{:S(2)}) %collective-permute-start.7) | collective-permute-done | bytes 6464 | tf_op jit(solution)/shard_map/ppermute | solution.py:27
  87.8 1.4 broadcast_multiply_fusion.7
  89.2 2.2 %broadcast_multiply_fusion.5 = (f32[4,134,262]{2,1,0:T(8,128)S(1)}, f32[4,134,262]{2,1,0:T(8,128)S(1)}, f32[4,134,262]{2,1,0:T(8,128)S(1)}, f32[4,134,262]{2,1,0:T(8,128)S(1)}) fusion(f32[134,262]{1,0:T(8,128)S(1)} %get-tuple-element.48, f32[4,134,3]{2,1,0:T(8,128)} %collective-permute-done.7, f32[4,3,256]{2,1,0:T(4,128)} %copy-done.2, ...), kind=kLoop, calls=%fused_computation.72 | loop fusion | flops 2527776 | bytes 4353392 | tf_op jit(solution)/shard_map/mul | solution.py:121
  92.6 1.8 multiply_add_fusion.5
  94.5 1.9 collective-permute-start.16
  96.5 4.5 %collective-permute-start.17 = (f32[4,1,256]{2,1,0:T(1,128)S(1)}, f32[4,1,256]{2,1,0:T(1,128)S(1)}, u32[]{:S(2)}, u32[]{:S(2)}) collective-permute-start(f32[4,1,256]{2,1,0:T(1,128)S(1)} %get-tuple-element.41), channel_id=1, source_target_pairs={{0,4},{4,8},{8,12},{12,16},{16,20},{20,24},{24,28},{1,5},{5,9},{9,... | collective-permute-start | bytes 12296 | tf_op jit(solution)/shard_map/ppermute | solution.py:26
  101.0 1.9 collective-permute-start.20
  103.0 4.5 %collective-permute-start.21 = (f32[4,1,256]{2,1,0:T(1,128)S(1)}, f32[4,1,256]{2,1,0:T(1,128)S(1)}, u32[]{:S(2)}, u32[]{:S(2)}) collective-permute-start(f32[4,1,256]{2,1,0:T(1,128)S(1)} %get-tuple-element.43), channel_id=1, source_target_pairs={{0,4},{4,8},{8,12},{12,16},{16,20},{20,24},{24,28},{1,5},{5,9},{9,... | collective-permute-start | bytes 12296 | tf_op jit(solution)/shard_map/ppermute | solution.py:26
  107.7 1.3 collective-permute-start.18
  109.0 4.0 %collective-permute-start.19 = (f32[4,130,1]{2,1,0:T(8,128)S(1)}, f32[4,130,1]{2,1,0:T(8,128)S(1)}, u32[]{:S(2)}, u32[]{:S(2)}) collective-permute-start(f32[4,130,1]{2,1,0:T(8,128)S(1)} %get-tuple-element.34), channel_id=1, source_target_pairs={{0,1},{1,2},{2,3},{4,5},{5,6},{6,7},{8,9},{9,10},{10,11},{12,13},{... | collective-permute-start | bytes 6248 | tf_op jit(solution)/shard_map/ppermute | solution.py:26
  113.3 1.3 collective-permute-start.22
  114.6 4.2 %collective-permute-start.23 = (f32[4,130,1]{2,1,0:T(8,128)S(1)}, f32[4,130,1]{2,1,0:T(8,128)S(1)}, u32[]{:S(2)}, u32[]{:S(2)}) collective-permute-start(f32[4,130,1]{2,1,0:T(8,128)S(1)} %get-tuple-element.38), channel_id=1, source_target_pairs={{0,1},{1,2},{2,3},{4,5},{5,6},{6,7},{8,9},{9,10},{10,11},{12,13},{... | collective-permute-start | bytes 6248 | tf_op jit(solution)/shard_map/ppermute | solution.py:26
  118.8 3.7 %collective-permute-done.22 = f32[4,130,1]{2,1,0:T(8,128)S(1)} collective-permute-done((f32[4,130,1]{2,1,0:T(8,128)S(1)}, f32[4,130,1]{2,1,0:T(8,128)S(1)}, u32[]{:S(2)}, u32[]{:S(2)}) %collective-permute-start.22) | collective-permute-done | bytes 2112 | tf_op jit(solution)/shard_map/ppermute | solution.py:27
  122.4 1.8 collective-permute-done.23
  124.2 1.1 fusion.9
  125.3 18.6 %reshape.48 = f32[4,32,4,64,4]{4,3,2,1,0:T(8,128)} reshape(f32[4,128,256]{2,1,0:T(8,128)S(1)} %get-tuple-element.16) | data formatting | bytes 1048576 | tf_op jit(solution)/shard_map/reshape | solution.py:58
  143.9 7.1 %reduce_sum.28 = f32[4,32,64]{2,1,0:T(8,128)S(1)} reduce(f32[4,32,4,64,4]{4,3,2,1,0:T(8,128)} %reshape.48, f32[]{:T(128)} %constant.29.clone.1), dimensions={2,4}, to_apply=%region_2.3 | reduce | flops 122880 | bytes 557060 | tf_op jit(solution)/shard_map/reduce_sum | solution.py:59
  151.1 3.8 %collective-permute-start.28 = (f32[4,32,3]{2,1,0:T(8,128)S(1)}, f32[4,32,3]{2,1,0:T(8,128)S(1)}, u32[]{:S(2)}, u32[]{:S(2)}) collective-permute-start(f32[4,32,3]{2,1,0:T(8,128)S(1)} %get-tuple-element.67), channel_id=1, source_target_pairs={{0,1},{1,2},{2,3},{4,5},{5,6},{6,7},{8,9},{9,10},{10,11},{12,13},{... | collective-permute-start | bytes 4616 | tf_op jit(solution)/shard_map/ppermute | solution.py:26
  154.9 1.3 collective-permute-start.29
  156.5 3.8 %collective-permute-done.29 = f32[4,32,3]{2,1,0:T(8,128)S(1)} collective-permute-done((f32[4,32,3]{2,1,0:T(8,128)S(1)}, f32[4,32,3]{2,1,0:T(8,128)S(1)}, u32[]{:S(2)}, u32[]{:S(2)}) %collective-permute-start.29) | collective-permute-done | bytes 1568 | tf_op jit(solution)/shard_map/ppermute | solution.py:27
  160.4 2.9 %collective-permute-start.30 = (f32[4,1,70]{2,1,0:T(1,128)S(1)}, f32[4,1,70]{2,1,0:T(1,128)S(1)}, u32[]{:S(2)}, u32[]{:S(2)}) collective-permute-start(f32[4,1,70]{2,1,0:T(1,128)S(1)} %get-tuple-element.66), channel_id=1, source_target_pairs={{4,0},{8,4},{12,8},{16,12},{20,16},{24,20},{28,24},{5,1},{9,5},{13... | collective-permute-start | bytes 3368 | tf_op jit(solution)/shard_map/ppermute | solution.py:27
  163.4 3.5 %collective-permute-start.31 = (f32[4,1,70]{2,1,0:T(1,128)S(1)}, f32[4,1,70]{2,1,0:T(1,128)S(1)}, u32[]{:S(2)}, u32[]{:S(2)}) collective-permute-start(f32[4,1,70]{2,1,0:T(1,128)S(1)} %get-tuple-element.65), channel_id=1, source_target_pairs={{0,4},{4,8},{8,12},{12,16},{16,20},{20,24},{24,28},{1,5},{5,9},{9,... | collective-permute-start | bytes 3368 | tf_op jit(solution)/shard_map/ppermute | solution.py:26
  167.8 2.6 %collective-permute-start.32 = (f32[4,1,70]{2,1,0:T(1,128)S(1)}, f32[4,1,70]{2,1,0:T(1,128)S(1)}, u32[]{:S(2)}, u32[]{:S(2)}) collective-permute-start(f32[4,1,70]{2,1,0:T(1,128)S(1)} %get-tuple-element.64), channel_id=1, source_target_pairs={{4,0},{8,4},{12,8},{16,12},{20,16},{24,20},{28,24},{5,1},{9,5},{13... | collective-permute-start | bytes 3368 | tf_op jit(solution)/shard_map/ppermute | solution.py:27
  170.4 4.4 %collective-permute-start.33 = (f32[4,1,70]{2,1,0:T(1,128)S(1)}, f32[4,1,70]{2,1,0:T(1,128)S(1)}, u32[]{:S(2)}, u32[]{:S(2)}) collective-permute-start(f32[4,1,70]{2,1,0:T(1,128)S(1)} %get-tuple-element.63), channel_id=1, source_target_pairs={{0,4},{4,8},{8,12},{12,16},{16,20},{20,24},{24,28},{1,5},{5,9},{9,... | collective-permute-start | bytes 3368 | tf_op jit(solution)/shard_map/ppermute | solution.py:26
  175.8 1.9 collective-permute-start.34
  177.7 5.1 %collective-permute-start.35 = (f32[4,1,70]{2,1,0:T(1,128)S(1)}, f32[4,1,70]{2,1,0:T(1,128)S(1)}, u32[]{:S(2)}, u32[]{:S(2)}) collective-permute-start(f32[4,1,70]{2,1,0:T(1,128)S(1)} %get-tuple-element.61), channel_id=1, source_target_pairs={{0,4},{4,8},{8,12},{12,16},{16,20},{20,24},{24,28},{1,5},{5,9},{9,... | collective-permute-start | bytes 3368 | tf_op jit(solution)/shard_map/ppermute | solution.py:26
  182.8 2.4 %collective-permute-start.24 = (f32[4,3,256]{2,1,0:T(4,128)S(1)}, f32[4,3,256]{2,1,0:T(4,128)S(1)}, u32[]{:S(2)}, u32[]{:S(2)}) collective-permute-start(f32[4,3,256]{2,1,0:T(4,128)S(1)} %get-tuple-element.39), channel_id=1, source_target_pairs={{0,4},{4,8},{8,12},{12,16},{16,20},{20,24},{24,28},{1,5},{5,9},{9,... | collective-permute-start | bytes 36872 | tf_op jit(solution)/shard_map/ppermute | solution.py:26
  185.2 1.9 collective-permute-start.25
  187.4 3.8 %collective-permute-done.25 = f32[4,3,256]{2,1,0:T(4,128)S(1)} collective-permute-done((f32[4,3,256]{2,1,0:T(4,128)S(1)}, f32[4,3,256]{2,1,0:T(4,128)S(1)}, u32[]{:S(2)}, u32[]{:S(2)}) %collective-permute-start.25) | collective-permute-done | bytes 12320 | tf_op jit(solution)/shard_map/ppermute | solution.py:27
  191.3 0.9 fusion.66
  192.2 2.9 %collective-permute-start.26 = (f32[4,134,3]{2,1,0:T(8,128)}, f32[4,134,3]{2,1,0:T(8,128)}, u32[]{:S(2)}, u32[]{:S(2)}) collective-permute-start(f32[4,134,3]{2,1,0:T(8,128)} %get-tuple-element.31), channel_id=1, source_target_pairs={{0,1},{1,2},{2,3},{4,5},{5,6},{6,7},{8,9},{9,10},{10,11},{12,13},{... | collective-permute-start | bytes 19304 | tf_op jit(solution)/shard_map/ppermute | solution.py:26
  195.1 1.3 collective-permute-start.27
  197.0 2.0 collective-permute-done.26
  199.0 4.8 %collective-permute-done.27 = f32[4,134,3]{2,1,0:T(8,128)} collective-permute-done((f32[4,134,3]{2,1,0:T(8,128)}, f32[4,134,3]{2,1,0:T(8,128)}, u32[]{:S(2)}, u32[]{:S(2)}) %collective-permute-start.27) | collective-permute-done | bytes 6464 | tf_op jit(solution)/shard_map/ppermute | solution.py:27
  203.8 1.5 broadcast_multiply_fusion.6
  205.3 1.9 broadcast_multiply_fusion.2
  208.5 1.8 fusion.2
  (112 shorter events, 10.8 us)
Async XLA Ops:
  0.9 14.0 %collective-permute-start = (s32[4,256]{1,0:T(4,128)S(1)}, s32[4,256]{1,0:T(4,128)S(1)}, u32[]{:S(2)}, u32[]{:S(2)}) collective-permute-start(s32[4,256]{1,0:T(4,128)S(1)} %get-tuple-element.55), channel_id=1, source_target_pairs={{0,4},{4,8},{8,12},{12,16},{16,20},{20,24},{24,28},{1,5},{5,9},{9,... | collective-permute-start | bytes 12296 | tf_op jit(solution)/shard_map/ppermute | solution.py:26
  4.6 10.3 %collective-permute-start.1 = (s32[4,256]{1,0:T(4,128)S(1)}, s32[4,256]{1,0:T(4,128)S(1)}, u32[]{:S(2)}, u32[]{:S(2)}) collective-permute-start(s32[4,256]{1,0:T(4,128)S(1)} %get-tuple-element.56), channel_id=1, source_target_pairs={{4,0},{8,4},{12,8},{16,12},{20,16},{24,20},{28,24},{5,1},{9,5},{13... | collective-permute-start | bytes 12296 | tf_op jit(solution)/shard_map/ppermute | solution.py:27
  15.0 4.6 %collective-permute-start.2 = (s32[136,4]{1,0:T(8,128)S(1)}, s32[136,4]{1,0:T(8,128)S(1)}, u32[]{:S(2)}, u32[]{:S(2)}) collective-permute-start(s32[136,4]{1,0:T(8,128)S(1)} %get-tuple-element.51), channel_id=1, source_target_pairs={{0,1},{1,2},{2,3},{4,5},{5,6},{6,7},{8,9},{9,10},{10,11},{12,13},{... | collective-permute-start | bytes 6536 | tf_op jit(solution)/shard_map/ppermute | solution.py:26
  18.2 5.1 %collective-permute-start.3 = (s32[136,4]{1,0:T(8,128)S(1)}, s32[136,4]{1,0:T(8,128)S(1)}, u32[]{:S(2)}, u32[]{:S(2)}) collective-permute-start(s32[136,4]{1,0:T(8,128)S(1)} %get-tuple-element.52), channel_id=1, source_target_pairs={{1,0},{2,1},{3,2},{5,4},{6,5},{7,6},{9,8},{10,9},{11,10},{13,12},{... | collective-permute-start | bytes 6536 | tf_op jit(solution)/shard_map/ppermute | solution.py:27
  32.8 4.5 %collective-permute-start.8 = (f32[4,32,3]{2,1,0:T(8,128)S(1)}, f32[4,32,3]{2,1,0:T(8,128)S(1)}, u32[]{:S(2)}, u32[]{:S(2)}) collective-permute-start(f32[4,32,3]{2,1,0:T(8,128)S(1)} %reduce_sum.25), channel_id=1, source_target_pairs={{0,1},{1,2},{2,3},{4,5},{5,6},{6,7},{8,9},{9,10},{10,11},{12,13},{... | collective-permute-start | bytes 4616 | tf_op jit(solution)/shard_map/ppermute | solution.py:26
  36.0 5.0 %collective-permute-start.9 = (f32[4,32,3]{2,1,0:T(8,128)S(1)}, f32[4,32,3]{2,1,0:T(8,128)S(1)}, u32[]{:S(2)}, u32[]{:S(2)}) collective-permute-start(f32[4,32,3]{2,1,0:T(8,128)S(1)} %reduce_sum.27), channel_id=1, source_target_pairs={{1,0},{2,1},{3,2},{5,4},{6,5},{7,6},{9,8},{10,9},{11,10},{13,12},{... | collective-permute-start | bytes 4616 | tf_op jit(solution)/shard_map/ppermute | solution.py:27
  37.3 16.3 %copy-start.5 = (f32[70]{0:T(128)}, f32[70]{0:T(128)S(1)}, u32[]{:S(2)}) copy-start(f32[70]{0:T(128)S(1)} %broadcast_select_fusion) | copy-start | bytes 844
  41.2 10.1 %collective-permute-start.10 = (f32[4,1,70]{2,1,0:T(1,128)S(1)}, f32[4,1,70]{2,1,0:T(1,128)S(1)}, u32[]{:S(2)}, u32[]{:S(2)}) collective-permute-start(f32[4,1,70]{2,1,0:T(1,128)S(1)} %get-tuple-element.74), channel_id=1, source_target_pairs={{4,0},{8,4},{12,8},{16,12},{20,16},{24,20},{28,24},{5,1},{9,5},{13... | collective-permute-start | bytes 3368 | tf_op jit(solution)/shard_map/ppermute | solution.py:27
  46.6 4.7 %collective-permute-start.11 = (f32[4,1,70]{2,1,0:T(1,128)S(1)}, f32[4,1,70]{2,1,0:T(1,128)S(1)}, u32[]{:S(2)}, u32[]{:S(2)}) collective-permute-start(f32[4,1,70]{2,1,0:T(1,128)S(1)} %get-tuple-element.73), channel_id=1, source_target_pairs={{0,4},{4,8},{8,12},{12,16},{16,20},{20,24},{24,28},{1,5},{5,9},{9,... | collective-permute-start | bytes 3368 | tf_op jit(solution)/shard_map/ppermute | solution.py:26
  51.2 29.6 %copy-start.3 = (f32[64]{0:T(128)}, f32[64]{0:T(128)S(1)}, u32[]{:S(2)}) copy-start(f32[64]{0:T(128)S(1)} %slice.489) | copy-start | bytes 772
  51.4 8.1 %collective-permute-start.12 = (f32[4,1,70]{2,1,0:T(1,128)S(1)}, f32[4,1,70]{2,1,0:T(1,128)S(1)}, u32[]{:S(2)}, u32[]{:S(2)}) collective-permute-start(f32[4,1,70]{2,1,0:T(1,128)S(1)} %get-tuple-element.72), channel_id=1, source_target_pairs={{4,0},{8,4},{12,8},{16,12},{20,16},{24,20},{28,24},{5,1},{9,5},{13... | collective-permute-start | bytes 3368 | tf_op jit(solution)/shard_map/ppermute | solution.py:27
  53.6 5.9 %collective-permute-start.13 = (f32[4,1,70]{2,1,0:T(1,128)S(1)}, f32[4,1,70]{2,1,0:T(1,128)S(1)}, u32[]{:S(2)}, u32[]{:S(2)}) collective-permute-start(f32[4,1,70]{2,1,0:T(1,128)S(1)} %get-tuple-element.71), channel_id=1, source_target_pairs={{0,4},{4,8},{8,12},{12,16},{16,20},{20,24},{24,28},{1,5},{5,9},{9,... | collective-permute-start | bytes 3368 | tf_op jit(solution)/shard_map/ppermute | solution.py:26
  59.8 11.0 %collective-permute-start.14 = (f32[4,1,70]{2,1,0:T(1,128)S(1)}, f32[4,1,70]{2,1,0:T(1,128)S(1)}, u32[]{:S(2)}, u32[]{:S(2)}) collective-permute-start(f32[4,1,70]{2,1,0:T(1,128)S(1)} %get-tuple-element.70), channel_id=1, source_target_pairs={{4,0},{8,4},{12,8},{16,12},{20,16},{24,20},{28,24},{5,1},{9,5},{13... | collective-permute-start | bytes 3368 | tf_op jit(solution)/shard_map/ppermute | solution.py:27
  61.7 9.1 %collective-permute-start.15 = (f32[4,1,70]{2,1,0:T(1,128)S(1)}, f32[4,1,70]{2,1,0:T(1,128)S(1)}, u32[]{:S(2)}, u32[]{:S(2)}) collective-permute-start(f32[4,1,70]{2,1,0:T(1,128)S(1)} %get-tuple-element.69), channel_id=1, source_target_pairs={{0,4},{4,8},{8,12},{12,16},{16,20},{20,24},{24,28},{1,5},{5,9},{9,... | collective-permute-start | bytes 3368 | tf_op jit(solution)/shard_map/ppermute | solution.py:26
  66.4 4.6 %collective-permute-start.4 = (f32[4,3,256]{2,1,0:T(4,128)S(1)}, f32[4,3,256]{2,1,0:T(4,128)S(1)}, u32[]{:S(2)}, u32[]{:S(2)}) collective-permute-start(f32[4,3,256]{2,1,0:T(4,128)S(1)} %broadcast_in_dim.31), channel_id=1, source_target_pairs={{0,4},{4,8},{8,12},{12,16},{16,20},{20,24},{24,28},{1,5},{5,9},{9,... | collective-permute-start | bytes 36872 | tf_op jit(solution)/shard_map/ppermute | solution.py:26
  68.9 6.0 %collective-permute-start.5 = (f32[4,3,256]{2,1,0:T(4,128)S(1)}, f32[4,3,256]{2,1,0:T(4,128)S(1)}, u32[]{:S(2)}, u32[]{:S(2)}) collective-permute-start(f32[4,3,256]{2,1,0:T(4,128)S(1)} %broadcast_in_dim.33), channel_id=1, source_target_pairs={{4,0},{8,4},{12,8},{16,12},{20,16},{24,20},{28,24},{5,1},{9,5},{13... | collective-permute-start | bytes 36872 | tf_op jit(solution)/shard_map/ppermute | solution.py:27
  74.8 14.4 %copy-start.2 = (f32[4,3,256]{2,1,0:T(4,128)}, f32[4,3,256]{2,1,0:T(4,128)S(1)}, u32[]{:S(2)}) copy-start(f32[4,3,256]{2,1,0:T(4,128)S(1)} %collective-permute-done.5) | copy-start | bytes 36868
  75.8 7.8 %collective-permute-start.6 = (f32[4,134,3]{2,1,0:T(8,128)}, f32[4,134,3]{2,1,0:T(8,128)S(1)}, u32[]{:S(2)}, u32[]{:S(2)}) collective-permute-start(f32[4,134,3]{2,1,0:T(8,128)} %get-tuple-element.35), channel_id=1, source_target_pairs={{0,1},{1,2},{2,3},{4,5},{5,6},{6,7},{8,9},{9,10},{10,11},{12,13},{... | collective-permute-start | bytes 19304 | tf_op jit(solution)/shard_map/ppermute | solution.py:26
  79.1 8.7 %collective-permute-start.7 = (f32[4,134,3]{2,1,0:T(8,128)}, f32[4,134,3]{2,1,0:T(8,128)}, u32[]{:S(2)}, u32[]{:S(2)}) collective-permute-start(f32[4,134,3]{2,1,0:T(8,128)} %get-tuple-element.36), channel_id=1, source_target_pairs={{1,0},{2,1},{3,2},{5,4},{6,5},{7,6},{9,8},{10,9},{11,10},{13,12},{... | collective-permute-start | bytes 19304 | tf_op jit(solution)/shard_map/ppermute | solution.py:27
  83.7 5.5 %copy-start.1 = (f32[4,134,3]{2,1,0:T(8,128)}, f32[4,134,3]{2,1,0:T(8,128)S(1)}, u32[]{:S(2)}) copy-start(f32[4,134,3]{2,1,0:T(8,128)S(1)} %collective-permute-done.6) | copy-start | bytes 19300
  94.5 13.0 %collective-permute-start.16 = (f32[4,1,256]{2,1,0:T(1,128)S(1)}, f32[4,1,256]{2,1,0:T(1,128)S(1)}, u32[]{:S(2)}, u32[]{:S(2)}) collective-permute-start(f32[4,1,256]{2,1,0:T(1,128)S(1)} %get-tuple-element.42), channel_id=1, source_target_pairs={{4,0},{8,4},{12,8},{16,12},{20,16},{24,20},{28,24},{5,1},{9,5},{13... | collective-permute-start | bytes 12296 | tf_op jit(solution)/shard_map/ppermute | solution.py:27
  96.5 11.1 %collective-permute-start.17 = (f32[4,1,256]{2,1,0:T(1,128)S(1)}, f32[4,1,256]{2,1,0:T(1,128)S(1)}, u32[]{:S(2)}, u32[]{:S(2)}) collective-permute-start(f32[4,1,256]{2,1,0:T(1,128)S(1)} %get-tuple-element.41), channel_id=1, source_target_pairs={{0,4},{4,8},{8,12},{12,16},{16,20},{20,24},{24,28},{1,5},{5,9},{9,... | collective-permute-start | bytes 12296 | tf_op jit(solution)/shard_map/ppermute | solution.py:26
  101.0 12.0 %collective-permute-start.20 = (f32[4,1,256]{2,1,0:T(1,128)S(1)}, f32[4,1,256]{2,1,0:T(1,128)S(1)}, u32[]{:S(2)}, u32[]{:S(2)}) collective-permute-start(f32[4,1,256]{2,1,0:T(1,128)S(1)} %get-tuple-element.44), channel_id=1, source_target_pairs={{4,0},{8,4},{12,8},{16,12},{20,16},{24,20},{28,24},{5,1},{9,5},{13... | collective-permute-start | bytes 12296 | tf_op jit(solution)/shard_map/ppermute | solution.py:27
  103.0 10.1 %collective-permute-start.21 = (f32[4,1,256]{2,1,0:T(1,128)S(1)}, f32[4,1,256]{2,1,0:T(1,128)S(1)}, u32[]{:S(2)}, u32[]{:S(2)}) collective-permute-start(f32[4,1,256]{2,1,0:T(1,128)S(1)} %get-tuple-element.43), channel_id=1, source_target_pairs={{0,4},{4,8},{8,12},{12,16},{16,20},{20,24},{24,28},{1,5},{5,9},{9,... | collective-permute-start | bytes 12296 | tf_op jit(solution)/shard_map/ppermute | solution.py:26
  107.7 11.0 %collective-permute-start.18 = (f32[4,130,1]{2,1,0:T(8,128)S(1)}, f32[4,130,1]{2,1,0:T(8,128)S(1)}, u32[]{:S(2)}, u32[]{:S(2)}) collective-permute-start(f32[4,130,1]{2,1,0:T(8,128)S(1)} %get-tuple-element.33), channel_id=1, source_target_pairs={{1,0},{2,1},{3,2},{5,4},{6,5},{7,6},{9,8},{10,9},{11,10},{13,12},{... | collective-permute-start | bytes 6248 | tf_op jit(solution)/shard_map/ppermute | solution.py:27
  109.0 9.7 %collective-permute-start.19 = (f32[4,130,1]{2,1,0:T(8,128)S(1)}, f32[4,130,1]{2,1,0:T(8,128)S(1)}, u32[]{:S(2)}, u32[]{:S(2)}) collective-permute-start(f32[4,130,1]{2,1,0:T(8,128)S(1)} %get-tuple-element.34), channel_id=1, source_target_pairs={{0,1},{1,2},{2,3},{4,5},{5,6},{6,7},{8,9},{9,10},{10,11},{12,13},{... | collective-permute-start | bytes 6248 | tf_op jit(solution)/shard_map/ppermute | solution.py:26
  113.3 9.2 %collective-permute-start.22 = (f32[4,130,1]{2,1,0:T(8,128)S(1)}, f32[4,130,1]{2,1,0:T(8,128)S(1)}, u32[]{:S(2)}, u32[]{:S(2)}) collective-permute-start(f32[4,130,1]{2,1,0:T(8,128)S(1)} %get-tuple-element.37), channel_id=1, source_target_pairs={{1,0},{2,1},{3,2},{5,4},{6,5},{7,6},{9,8},{10,9},{11,10},{13,12},{... | collective-permute-start | bytes 6248 | tf_op jit(solution)/shard_map/ppermute | solution.py:27
  114.6 9.6 %collective-permute-start.23 = (f32[4,130,1]{2,1,0:T(8,128)S(1)}, f32[4,130,1]{2,1,0:T(8,128)S(1)}, u32[]{:S(2)}, u32[]{:S(2)}) collective-permute-start(f32[4,130,1]{2,1,0:T(8,128)S(1)} %get-tuple-element.38), channel_id=1, source_target_pairs={{0,1},{1,2},{2,3},{4,5},{5,6},{6,7},{8,9},{9,10},{10,11},{12,13},{... | collective-permute-start | bytes 6248 | tf_op jit(solution)/shard_map/ppermute | solution.py:26
  125.3 35.0 %copy-start.6 = (f32[70]{0:T(128)S(1)}, f32[70]{0:T(128)}, u32[]{:S(2)}) copy-start(f32[70]{0:T(128)} %copy-done.5) | copy-start | bytes 844
  125.3 71.1 %copy-start.4 = (f32[64]{0:T(128)S(1)}, f32[64]{0:T(128)}, u32[]{:S(2)}) copy-start(f32[64]{0:T(128)} %copy-done.3) | copy-start | bytes 772
  143.9 64.5 %copy-start = (f32[4,128,256]{2,1,0:T(8,128)S(1)}, f32[4,128,256]{2,1,0:T(8,128)}, u32[]{:S(2)}) copy-start(f32[4,128,256]{2,1,0:T(8,128)} %get-tuple-element.10) | copy-start | bytes 1572868
  151.1 5.4 %collective-permute-start.28 = (f32[4,32,3]{2,1,0:T(8,128)S(1)}, f32[4,32,3]{2,1,0:T(8,128)S(1)}, u32[]{:S(2)}, u32[]{:S(2)}) collective-permute-start(f32[4,32,3]{2,1,0:T(8,128)S(1)} %get-tuple-element.67), channel_id=1, source_target_pairs={{0,1},{1,2},{2,3},{4,5},{5,6},{6,7},{8,9},{9,10},{10,11},{12,13},{... | collective-permute-start | bytes 4616 | tf_op jit(solution)/shard_map/ppermute | solution.py:26
  154.9 5.4 %collective-permute-start.29 = (f32[4,32,3]{2,1,0:T(8,128)S(1)}, f32[4,32,3]{2,1,0:T(8,128)S(1)}, u32[]{:S(2)}, u32[]{:S(2)}) collective-permute-start(f32[4,32,3]{2,1,0:T(8,128)S(1)} %get-tuple-element.68), channel_id=1, source_target_pairs={{1,0},{2,1},{3,2},{5,4},{6,5},{7,6},{9,8},{10,9},{11,10},{13,12},{... | collective-permute-start | bytes 4616 | tf_op jit(solution)/shard_map/ppermute | solution.py:27
  160.4 6.5 %collective-permute-start.30 = (f32[4,1,70]{2,1,0:T(1,128)S(1)}, f32[4,1,70]{2,1,0:T(1,128)S(1)}, u32[]{:S(2)}, u32[]{:S(2)}) collective-permute-start(f32[4,1,70]{2,1,0:T(1,128)S(1)} %get-tuple-element.66), channel_id=1, source_target_pairs={{4,0},{8,4},{12,8},{16,12},{20,16},{24,20},{28,24},{5,1},{9,5},{13... | collective-permute-start | bytes 3368 | tf_op jit(solution)/shard_map/ppermute | solution.py:27
  163.4 4.3 %collective-permute-start.31 = (f32[4,1,70]{2,1,0:T(1,128)S(1)}, f32[4,1,70]{2,1,0:T(1,128)S(1)}, u32[]{:S(2)}, u32[]{:S(2)}) collective-permute-start(f32[4,1,70]{2,1,0:T(1,128)S(1)} %get-tuple-element.65), channel_id=1, source_target_pairs={{0,4},{4,8},{8,12},{12,16},{16,20},{20,24},{24,28},{1,5},{5,9},{9,... | collective-permute-start | bytes 3368 | tf_op jit(solution)/shard_map/ppermute | solution.py:26
  167.8 7.0 %collective-permute-start.32 = (f32[4,1,70]{2,1,0:T(1,128)S(1)}, f32[4,1,70]{2,1,0:T(1,128)S(1)}, u32[]{:S(2)}, u32[]{:S(2)}) collective-permute-start(f32[4,1,70]{2,1,0:T(1,128)S(1)} %get-tuple-element.64), channel_id=1, source_target_pairs={{4,0},{8,4},{12,8},{16,12},{20,16},{24,20},{28,24},{5,1},{9,5},{13... | collective-permute-start | bytes 3368 | tf_op jit(solution)/shard_map/ppermute | solution.py:27
  170.4 5.2 %collective-permute-start.33 = (f32[4,1,70]{2,1,0:T(1,128)S(1)}, f32[4,1,70]{2,1,0:T(1,128)S(1)}, u32[]{:S(2)}, u32[]{:S(2)}) collective-permute-start(f32[4,1,70]{2,1,0:T(1,128)S(1)} %get-tuple-element.63), channel_id=1, source_target_pairs={{0,4},{4,8},{8,12},{12,16},{16,20},{20,24},{24,28},{1,5},{5,9},{9,... | collective-permute-start | bytes 3368 | tf_op jit(solution)/shard_map/ppermute | solution.py:26
  175.8 11.4 %collective-permute-start.34 = (f32[4,1,70]{2,1,0:T(1,128)S(1)}, f32[4,1,70]{2,1,0:T(1,128)S(1)}, u32[]{:S(2)}, u32[]{:S(2)}) collective-permute-start(f32[4,1,70]{2,1,0:T(1,128)S(1)} %get-tuple-element.62), channel_id=1, source_target_pairs={{4,0},{8,4},{12,8},{16,12},{20,16},{24,20},{28,24},{5,1},{9,5},{13... | collective-permute-start | bytes 3368 | tf_op jit(solution)/shard_map/ppermute | solution.py:27
  177.7 9.5 %collective-permute-start.35 = (f32[4,1,70]{2,1,0:T(1,128)S(1)}, f32[4,1,70]{2,1,0:T(1,128)S(1)}, u32[]{:S(2)}, u32[]{:S(2)}) collective-permute-start(f32[4,1,70]{2,1,0:T(1,128)S(1)} %get-tuple-element.61), channel_id=1, source_target_pairs={{0,4},{4,8},{8,12},{12,16},{16,20},{20,24},{24,28},{1,5},{5,9},{9,... | collective-permute-start | bytes 3368 | tf_op jit(solution)/shard_map/ppermute | solution.py:26
  182.8 4.6 %collective-permute-start.24 = (f32[4,3,256]{2,1,0:T(4,128)S(1)}, f32[4,3,256]{2,1,0:T(4,128)S(1)}, u32[]{:S(2)}, u32[]{:S(2)}) collective-permute-start(f32[4,3,256]{2,1,0:T(4,128)S(1)} %get-tuple-element.39), channel_id=1, source_target_pairs={{0,4},{4,8},{8,12},{12,16},{16,20},{20,24},{24,28},{1,5},{5,9},{9,... | collective-permute-start | bytes 36872 | tf_op jit(solution)/shard_map/ppermute | solution.py:26
  185.2 6.0 %collective-permute-start.25 = (f32[4,3,256]{2,1,0:T(4,128)S(1)}, f32[4,3,256]{2,1,0:T(4,128)S(1)}, u32[]{:S(2)}, u32[]{:S(2)}) collective-permute-start(f32[4,3,256]{2,1,0:T(4,128)S(1)} %get-tuple-element.40), channel_id=1, source_target_pairs={{4,0},{8,4},{12,8},{16,12},{20,16},{24,20},{28,24},{5,1},{9,5},{13... | collective-permute-start | bytes 36872 | tf_op jit(solution)/shard_map/ppermute | solution.py:27
  192.2 6.8 %collective-permute-start.26 = (f32[4,134,3]{2,1,0:T(8,128)}, f32[4,134,3]{2,1,0:T(8,128)}, u32[]{:S(2)}, u32[]{:S(2)}) collective-permute-start(f32[4,134,3]{2,1,0:T(8,128)} %get-tuple-element.31), channel_id=1, source_target_pairs={{0,1},{1,2},{2,3},{4,5},{5,6},{6,7},{8,9},{9,10},{10,11},{12,13},{... | collective-permute-start | bytes 19304 | tf_op jit(solution)/shard_map/ppermute | solution.py:26
  195.1 8.7 %collective-permute-start.27 = (f32[4,134,3]{2,1,0:T(8,128)}, f32[4,134,3]{2,1,0:T(8,128)}, u32[]{:S(2)}, u32[]{:S(2)}) collective-permute-start(f32[4,134,3]{2,1,0:T(8,128)} %get-tuple-element.32), channel_id=1, source_target_pairs={{1,0},{2,1},{3,2},{5,4},{6,5},{7,6},{9,8},{10,9},{11,10},{13,12},{... | collective-permute-start | bytes 19304 | tf_op jit(solution)/shard_map/ppermute | solution.py:27
where the time goes:
time: 212 us; the launch traced here: 210 us
  starting transfers between devices  104 us (49%)
  waiting for transfers between devices  39.6 us (19%)
  other arithmetic  37.2 us (18%)
  local copies, waits for them, and re-layouts  28.5 us (13%)
    ppermute x18, starting transfers between devices, with_halo(): before = lax.ppermute(last, axis, up)  68.6 us
    ppermute x18, starting transfers between devices, with_halo(): after = lax.ppermute(initial, axis, down)  35.5 us
    ppermute x18, waiting for transfers between devices, with_halo(): after = lax.ppermute(initial, axis, down)  31.4 us
    reshape x1, local copies, waits for them, and re-layouts, restrict(): residual.reshape(goals, height // COARSEN, COARSEN, width // COARSEN, COA...  18.6 us
    reduce_sum x2, other arithmetic, restrict(): return blocks.mean(axis=(2, 4))  9.61 us
    ppermute x18, waiting for transfers between devices, with_halo(): before = lax.ppermute(last, axis, up)  8.14 us
    unnamed x4, other arithmetic  7.52 us
    broadcast_in_dim x4, local copies, waits for them, and re-layouts, per_device(): source = jnp.broadcast_to(open_cells * load, (goals, tile_rows, tile_cols))  5.76 us
  transfers between devices with their start and end apart: 36, of which 14 were waited for; matrix products, arithmetic and copies ran while one was open for 6% of the time, Pallas kernels for 0%

commit v1 on v0

v1 whole, which is shorter than its diff:
```python
import functools

import jax
import jax.numpy as jnp
from jax import lax
from jax.experimental import pallas as pl
from jax.experimental.pallas import tpu as pltpu
from jax.sharding import PartitionSpec as P

COARSEN = 4
SMOOTH = 4
CSWEEPS = 4

SCREENING = 0.0001
EXIT_SINK = 4.0
COARSE_SHIFT = 0.01
DAMPING = 0.8
UPPER_BOUND = 12.5
LOWER_BOUND = 1.0

CENTER = 0.5 * (UPPER_BOUND + LOWER_BOUND)
LANES = 128
SUB = 8
HALO = COARSEN * CSWEEPS
COARSE_HALO = HALO // COARSEN

DIRECTIONS = ((-1, 0), (1, 0), (0, -1), (0, 1), (-1, -1), (-1, 1), (1, -1), (1, 1))


def smoother_coefficients():
    def add(p, q):
        size = max(len(p), len(q))
        p, q = p + [0.0] * (size - len(p)), q + [0.0] * (size - len(q))
        return [a + b for a, b in zip(p, q)]

    def scale(k, p):
        return [k * a for a in p]

    half_span = 0.5 * (UPPER_BOUND - LOWER_BOUND)
    sigma_ratio = CENTER / half_span
    ratio_old = 1.0 / sigma_ratio
    residual = [1.0]
    update = scale(1.0 / CENTER, residual)
    result = update
    for sweep in range(SMOOTH - 1):
        applied = scale(CENTER, add(update, scale(-1.0, [0.0] + update)))
        residual = add(residual, scale(-1.0, applied))
        ratio_new = 1.0 / (2.0 * sigma_ratio - ratio_old)
        update = add(
            scale(ratio_new * ratio_old, update), scale(2.0 * ratio_new / half_span, residual)
        )
        result = add(result, update)
        ratio_old = ratio_new
    return result


def lane_iota(rows):
    return lax.broadcasted_iota(jnp.int32, (rows, LANES), 1)


def exchange_kernel(
    peers, obst_ref, load_ref, out_ref, top, bot, lef, rig, from_rows, from_cols, from_corners,
    send_sem, recv_sem,
):
    rows, cols = obst_ref.shape
    tiles = cols // LANES
    me = (lax.axis_index("gx"), lax.axis_index("gy"))

    def exists(dx, dy):
        gx, gy = me[0] + dx, me[1] + dy
        return (gx >= 0) & (gx < peers[0]) & (gy >= 0) & (gy < peers[1])

    barrier = pltpu.get_barrier_semaphore()
    count = jnp.int32(0)
    for dx, dy in DIRECTIONS:
        there = exists(dx, dy)
        count = count + there.astype(jnp.int32)

        @pl.when(there)
        def _():
            pl.semaphore_signal(
                barrier, inc=1, device_id=(me[0] + dx, me[1] + dy),
                device_id_type=pl.DeviceIdType.MESH,
            )

    def source(start, size, tile):
        block = (pl.ds(start, size), pl.ds(tile * LANES, LANES))
        return (1 - obst_ref[block]).astype(jnp.float32) * load_ref[block]

    first = SUB + HALO
    for tile in range(tiles):
        top[tile] = source(0, HALO, tile)
        bot[tile] = source(rows - HALO, HALO, tile)
    lane = lane_iota(HALO)
    group = LANES // HALO
    for pack in range(rows // LANES):
        left = jnp.zeros((HALO, LANES), jnp.float32)
        right = jnp.zeros((HALO, LANES), jnp.float32)
        for b in range(group):
            start = pack * LANES + b * HALO
            here = (lane >= b * HALO) & (lane < (b + 1) * HALO)
            low = source(start, HALO, 0)
            high = source(start, HALO, tiles - 1)
            left = jnp.where(here, pltpu.roll(low, b * HALO, 1) if b else low, left)
            turn = ((b + 1) * HALO) % LANES
            right = jnp.where(here, pltpu.roll(high, turn, 1) if turn else high, right)
        lef[pl.ds(pack * HALO, HALO), :] = left
        rig[pl.ds(pack * HALO, HALO), :] = right

    messages = (
        (top, from_rows.at[0]),
        (bot, from_rows.at[1]),
        (lef, from_cols.at[0]),
        (rig, from_cols.at[1]),
        (top.at[0], from_corners.at[0]),
        (top.at[tiles - 1], from_corners.at[1]),
        (bot.at[0], from_corners.at[2]),
        (bot.at[tiles - 1], from_corners.at[3]),
    )

    def copy(k):
        dx, dy = DIRECTIONS[k]
        return pltpu.make_async_remote_copy(
            src_ref=messages[k][0], dst_ref=messages[k][1],
            send_sem=send_sem.at[k], recv_sem=recv_sem.at[k],
            device_id=(me[0] + dx, me[1] + dy), device_id_type=pl.DeviceIdType.MESH,
        )

    pl.semaphore_wait(barrier, count)
    order = (4, 5, 6, 7, 0, 1, 2, 3)
    for k in order:

        @pl.when(exists(*DIRECTIONS[k]))
        def _():
            copy(k).start()

    wide = rows + 2 * HALO
    for tile in range(tiles + 1):
        out_ref[tile, pl.ds(0, SUB), :] = jnp.zeros((SUB, LANES), jnp.float32)
        out_ref[tile, pl.ds(SUB + wide, SUB), :] = jnp.zeros((SUB, LANES), jnp.float32)
    for tile in range(tiles):
        out_ref[tile, pl.ds(first, rows), :] = source(0, rows, tile)

    for k in order:
        dx, dy = DIRECTIONS[k]

        @pl.when(exists(-dx, -dy))
        def _():
            copy(k).wait_recv()

        @pl.when(jnp.logical_not(exists(-dx, -dy)))
        def _():
            messages[k][1][...] = jnp.zeros(messages[k][1].shape, jnp.float32)

    for tile in range(tiles):
        out_ref[tile, pl.ds(first + rows, HALO), :] = from_rows[0, tile]
        out_ref[tile, pl.ds(SUB, HALO), :] = from_rows[1, tile]

    def rim(right, left):
        return jnp.where(lane < HALO, right, jnp.where(lane >= LANES - HALO, left, 0.0))

    out_ref[tiles, pl.ds(first + rows, HALO), :] = rim(from_corners[0], from_corners[1])
    out_ref[tiles, pl.ds(SUB, HALO), :] = rim(from_corners[2], from_corners[3])
    for pack in range(rows // LANES):
        right = from_cols[0, pl.ds(pack * HALO, HALO), :]
        left = from_cols[1, pl.ds(pack * HALO, HALO), :]
        for b in range(group):
            turn_right = (LANES - b * HALO) % LANES
            turn_left = (LANES - HALO - b * HALO) % LANES
            out_ref[tiles, pl.ds(first + pack * LANES + b * HALO, HALO), :] = rim(
                pltpu.roll(right, turn_right, 1) if turn_right else right,
                pltpu.roll(left, turn_left, 1) if turn_left else left,
            )

    for k in order:

        @pl.when(exists(*DIRECTIONS[k]))
        def _():
            copy(k).wait_send()


def cycles_kernel(
    peers, source_ref, exit_rows_ref, exit_cols_ref, out_ref,
    open_ref, marks_ref, diag_ref, first_ref, second_ref, rest_ref, shift_ref,
    expand_ref, corr_ref, fixed_ref, last_ref,
):
    goals, rows, cols = out_ref.shape
    tiles = cols // LANES
    span = tiles + 1
    ring = span * LANES
    wide = rows + 2 * HALO
    groups = wide // SUB
    coarse_rows = wide // COARSEN
    row_start = lax.axis_index("gx") * rows
    col_start = lax.axis_index("gy") * cols
    lane = lane_iota(SUB)
    sub = lax.broadcasted_iota(jnp.int32, (SUB, LANES), 0)
    coefficients = smoother_coefficients()
    inverse = 1.0 / CENTER

    def beside(center):
        up = [pltpu.roll(c, 1, 1) for c in center]
        down = [pltpu.roll(c, LANES - 1, 1) for c in center]
        return [
            jnp.where(lane == 0, up[t - 1], up[t])
            + jnp.where(lane == LANES - 1, down[(t + 1) % len(center)], down[t])
            for t in range(len(center))
        ]

    def load(ref, at, *lead):
        return [ref[(*lead, t, pl.ds(at, SUB), slice(None))] for t in range(span)]

    def cross(ref, at, *lead):
        center = load(ref, at, *lead)
        below = load(ref, at + 1, *lead)
        above = load(ref, at - 1, *lead)
        side = beside(center)
        return center, [below[t] + above[t] + side[t] for t in range(span)]

    def loop(low, high):
        def run(body):
            def step(i, carry):
                body(i, pl.multiple_of(i * SUB + SUB, SUB))
                return carry

            lax.fori_loop(low, high, step, 0)

        return run

    zero = jnp.zeros((SUB, LANES), jnp.float32)
    for ends in (0, wide + SUB):
        for t in range(span):
            open_ref[t, pl.ds(ends, SUB), :] = zero
            corr_ref[t, pl.ds(ends, SUB), :] = zero
            for g in range(goals):
                for ref in (first_ref, second_ref):
                    ref[g, t, pl.ds(ends, SUB), :] = zero

    @loop(0, groups)
    def _(i, at):
        for t in range(span):
            open_ref[t, pl.ds(at, SUB), :] = (source_ref[t, pl.ds(at, SUB), :] > 0.0).astype(
                jnp.float32
            )

    count = exit_rows_ref.shape[1]
    row_of = lax.broadcasted_iota(jnp.int32, (wide, count), 0) + (row_start - HALO)
    ring_lane = lax.broadcasted_iota(jnp.int32, (ring, count), 0)
    col_of = jnp.where(ring_lane < cols + LANES // 2, ring_lane, ring_lane - ring) + col_start
    for g in range(goals):
        row_hot = (row_of == exit_rows_ref[pl.ds(g, 1), :]).astype(jnp.float32)
        col_hot = (col_of == exit_cols_ref[pl.ds(g, 1), :]).astype(jnp.float32)
        marks = lax.dot_general(
            row_hot.astype(jnp.bfloat16), col_hot.astype(jnp.bfloat16),
            (((1,), (1,)), ((), ())), preferred_element_type=jnp.float32,
        )
        for t in range(span):
            marks_ref[g, t] = marks[:, t * LANES : (t + 1) * LANES]

    fine = lax.broadcasted_iota(jnp.int32, (ring, LANES), 0)
    fine = jnp.where(fine < cols + LANES // 2, fine, fine - ring + COARSEN * LANES) // COARSEN
    belongs = (fine == lax.broadcasted_iota(jnp.int32, (ring, LANES), 1)).astype(jnp.float32)

    def restrict(ref, offset, *lead):
        total = None
        for t in range(span):
            block = ref[(*lead, t, pl.ds(offset, coarse_rows, stride=COARSEN), slice(None))]
            for k in range(1, COARSEN):
                block = block + ref[
                    (*lead, t, pl.ds(offset + k, coarse_rows, stride=COARSEN), slice(None))
                ]
            part = lax.dot_general(
                block, belongs[t * LANES : (t + 1) * LANES], (((1,), (0,)), ((), ())),
                precision=lax.Precision.HIGHEST, preferred_element_type=jnp.float32,
            )
            total = part if total is None else total + part
        return total * (1.0 / (COARSEN * COARSEN))

    shape = (coarse_rows, LANES)
    coarse_row = lax.broadcasted_iota(jnp.int32, shape, 0) - COARSE_HALO + row_start // COARSEN
    coarse_lane = lax.broadcasted_iota(jnp.int32, shape, 1)
    coarse_col = (
        jnp.where(coarse_lane < cols // COARSEN + LANES // 8, coarse_lane, coarse_lane - LANES)
        + col_start // COARSEN
    )
    floor = (
        (coarse_row >= 0) & (coarse_row < peers[0] * rows // COARSEN)
        & (coarse_col >= 0) & (coarse_col < peers[1] * cols // COARSEN)
    ).astype(jnp.float32)

    def coarse_solve(rhs):
        center_weight = 4.0 + COARSE_SHIFT
        gain = DAMPING / center_weight
        estimate = gain * rhs * floor
        for sweep in range(CSWEEPS - 1):
            around = (
                pltpu.roll(estimate, coarse_rows - 1, 0) + pltpu.roll(estimate, 1, 0)
                + pltpu.roll(estimate, LANES - 1, 1) + pltpu.roll(estimate, 1, 1)
            )
            estimate = ((1.0 - DAMPING) * estimate + gain * (rhs + around)) * floor
        return estimate

    def widen(estimate, t):
        return lax.dot_general(
            estimate, belongs[t * LANES : (t + 1) * LANES], (((1,), (1,)), ((), ())),
            precision=lax.Precision.HIGHEST, preferred_element_type=jnp.float32,
        )

    def spread(ref, i, t, *lead):
        even = jnp.broadcast_to(ref[(*lead, t, pl.ds(2 * i, 1), slice(None))], (SUB, LANES))
        odd = jnp.broadcast_to(ref[(*lead, t, pl.ds(2 * i + 1, 1), slice(None))], (SUB, LANES))
        return jnp.where(sub < COARSEN, even, odd)

    estimate = coarse_solve(restrict(source_ref, SUB))
    for t in range(span):
        expand_ref[t] = widen(estimate, t)

    @loop(0, groups)
    def _(i, at):
        opened, around = cross(open_ref, at)
        source, source_around = cross(source_ref, at)
        for t in range(span):
            base = SCREENING + 4.0 * (1.0 - opened[t]) + opened[t] * around[t]
            mixed = (coefficients[3] * inverse) * opened[t] * source_around[t]
            mixed = mixed + coefficients[2] * source[t]
            lifted = coefficients[3] * source[t]
            sink = EXIT_SINK * opened[t]
            corr_ref[t, pl.ds(at, SUB), :] = opened[t] * spread(expand_ref, i, t)
            for g in range(goals):
                exits = jnp.minimum(marks_ref[g, t, pl.ds(i * SUB, SUB), :], 1.0)
                kept = 1.0 - (base + sink * exits) * inverse
                diag_ref[g, t, pl.ds(at, SUB), :] = kept
                first_ref[g, t, pl.ds(at, SUB), :] = kept * lifted + mixed

    def horner(old_ref, new_ref, coefficient, rhs):
        def body(i, at):
            weight = [inverse * open_ref[t, pl.ds(at, SUB), :] for t in range(span)]
            for g in range(goals):
                center, around = cross(old_ref, at, g)
                for t in range(span):
                    kept = diag_ref[g, t, pl.ds(at, SUB), :]
                    new_ref[g, t, pl.ds(at, SUB), :] = (
                        kept * center[t] + weight[t] * around[t] + coefficient * rhs(g, t, at)
                    )

        return body

    plain = lambda g, t, at: source_ref[t, pl.ds(at, SUB), :]
    loop(0, groups)(horner(first_ref, second_ref, coefficients[1], plain))
    loop(0, groups)(horner(second_ref, first_ref, coefficients[0], plain))

    @loop(0, groups)
    def _(i, at):
        correction, around_corr = cross(corr_ref, at)
        opened = load(open_ref, at)
        for g in range(goals):
            center, around = cross(first_ref, at, g)
            for t in range(span):
                kept = CENTER * (diag_ref[g, t, pl.ds(at, SUB), :] - 1.0)
                residual = (
                    source_ref[t, pl.ds(at, SUB), :] + kept * center[t] + opened[t] * around[t]
                )
                rest_ref[g, t, pl.ds(i * SUB, SUB), :] = residual
                shift_ref[g, t, pl.ds(at, SUB), :] = (
                    residual + kept * correction[t] + opened[t] * around_corr[t]
                )

    for g in range(goals):
        estimate = coarse_solve(restrict(rest_ref, 0, g))
        for t in range(tiles):
            last_ref[g, t] = widen(estimate, t)

    edge = HALO // SUB

    @loop(edge - 1, groups - edge + 1)
    def _(i, at):
        weight = [(coefficients[3] * inverse) * open_ref[t, pl.ds(at, SUB), :] for t in range(span)]
        for g in range(goals):
            center, around = cross(shift_ref, at, g)
            for t in range(span):
                kept = diag_ref[g, t, pl.ds(at, SUB), :]
                second_ref[g, t, pl.ds(at, SUB), :] = (
                    (coefficients[3] * kept + coefficients[2]) * center[t] + weight[t] * around[t]
                )

    shifted = lambda g, t, at: shift_ref[g, t, pl.ds(at, SUB), :]
    loop(edge - 1, groups - edge + 1)(horner(second_ref, fixed_ref, coefficients[1], shifted))

    @loop(edge, groups - edge)
    def _(i, at):
        opened = load(open_ref, at)
        for g in range(goals):
            center, around = cross(fixed_ref, at, g)
            for t in range(tiles):
                kept = diag_ref[g, t, pl.ds(at, SUB), :]
                smooth = (
                    kept * center[t] + (inverse * opened[t]) * around[t]
                    + coefficients[0] * shift_ref[g, t, pl.ds(at, SUB), :]
                )
                out_ref[g, pl.ds(pl.multiple_of(at - SUB - HALO, SUB), SUB), pl.ds(t * LANES, LANES)] = (
                    first_ref[g, t, pl.ds(at, SUB), :] + corr_ref[t, pl.ds(at, SUB), :]
                    + smooth + opened[t] * spread(last_ref, i, t, g)
                )


def per_device(peers, obstacles, load, exit_rows, exit_cols):
    rows, cols = obstacles.shape
    goals = exit_rows.shape[0]
    tiles = cols // LANES
    span = tiles + 1
    wide = rows + 2 * HALO
    padded = wide + 2 * SUB
    f32 = jnp.float32
    vmem = pl.BlockSpec(memory_space=pltpu.VMEM)
    packed = rows * HALO // LANES
    source = pl.pallas_call(
        functools.partial(exchange_kernel, peers),
        out_shape=jax.ShapeDtypeStruct((span, padded, LANES), f32),
        in_specs=[vmem] * 2,
        out_specs=vmem,
        scratch_shapes=[
            pltpu.VMEM((tiles, HALO, LANES), f32),
            pltpu.VMEM((tiles, HALO, LANES), f32),
            pltpu.VMEM((packed, LANES), f32),
            pltpu.VMEM((packed, LANES), f32),
            pltpu.VMEM((2, tiles, HALO, LANES), f32),
            pltpu.VMEM((2, packed, LANES), f32),
            pltpu.VMEM((4, HALO, LANES), f32),
            pltpu.SemaphoreType.DMA((len(DIRECTIONS),)),
            pltpu.SemaphoreType.DMA((len(DIRECTIONS),)),
        ],
        compiler_params=pltpu.CompilerParams(collective_id=0, has_side_effects=True),
        name="exchange",
    )(obstacles, load)
    field = pltpu.VMEM((goals, span, padded, LANES), f32)
    flat = pltpu.VMEM((goals, span, wide, LANES), f32)
    shared = pltpu.VMEM((span, padded, LANES), f32)
    coarse = wide // COARSEN
    return pl.pallas_call(
        functools.partial(cycles_kernel, peers),
        out_shape=jax.ShapeDtypeStruct((goals, rows, cols), f32),
        in_specs=[vmem] * 3,
        out_specs=vmem,
        scratch_shapes=[
            shared, flat, field, field, field, flat, field,
            pltpu.VMEM((span, coarse, LANES), f32), shared, field,
            pltpu.VMEM((goals, tiles, coarse, LANES), f32),
        ],
        compiler_params=pltpu.CompilerParams(vmem_limit_bytes=48 * 1024 * 1024),
        name="cycles",
    )(source, exit_rows, exit_cols)


def solution(mesh):
    peers = (mesh.shape["gx"], mesh.shape["gy"])
    return jax.shard_map(
        functools.partial(per_device, peers),
        mesh=mesh,
        in_specs=(P("gx", "gy"), P("gx", "gy"), P(), P()),
        out_specs=P(None, "gx", "gy"),
        check_vma=False,
    )
```

time: 212 us -> 28.9 us (0.14)
  the two profiles are of different devices: /device:TPU:3 before, /device:TPU:0 now
where the time goes in v1:
time: 28.9 us; the launch traced here: 28.7 us
  Pallas kernels  27.8 us (96%)
  local copies, waits for them, and re-layouts  0.95 us (3%)
    pallas_call x1, Pallas kernels, per_device(): pl.pallas_call(functools.partial(cycles_kernel, peers), out_shape=jax.Sha...  19.2 us
    pallas_call x1, Pallas kernels, per_device(): pl.pallas_call(functools.partial(exchange_kernel, peers), out_shape=jax.S...  8.54 us
    unnamed x6, local copies, waits for them, and re-layouts  0.95 us

profile of v1, /device:TPU:0, one launch (start us, length us, event | category | flops | bytes accessed | tf_op | source)
XLA Modules:
  0.0 28.7 jit_solution(10539796926887973393)
XLA Ops:
  0.0 0.0 copy-start.2
  0.0 0.0 copy-start.1
  0.0 8.5 %exchange.1.source_ref = f32[3,176,128]{2,1,0:T(8,128)} custom-call(s32[128,256]{1,0:T(8,128)} %obst_ref.1, f32[128,256]{1,0:T(8,128)} %load_ref.1), custom_call_target="tpu_custom_call" | custom-call | tf_op jit(solution)/shard_map/exchange/pallas_call | solution.py:416
  8.6 0.0 copy-done.2
  8.6 0.0 copy-done.1
  8.6 0.0 copy-start
  8.6 0.9 %copy-done = f32[3,176,128]{2,1,0:T(8,128)S(1)} copy-done((f32[3,176,128]{2,1,0:T(8,128)S(1)}, f32[3,176,128]{2,1,0:T(8,128)}, u32[]{:S(2)}) %copy-start) | copy-done | bytes 270360
  9.5 19.2 %cycles.1 = f32[4,128,256]{2,1,0:T(8,128)} custom-call(f32[3,176,128]{2,1,0:T(8,128)S(1)} %copy-done, s32[4,256]{1,0:T(4,128)S(1)} %copy-done.1, s32[4,256]{1,0:T(4,128)S(1)} %copy-done.2), custom_call_target="tpu_custom_call" | custom-call | tf_op jit(solution)/shard_map/cycles/pallas_call | solution.py:439
Async XLA Ops:
  0.0 8.6 %copy-start.2 = (s32[4,256]{1,0:T(4,128)S(1)}, s32[4,256]{1,0:T(4,128)}, u32[]{:S(2)}) copy-start(s32[4,256]{1,0:T(4,128)} %exit_cols_ref.1) | copy-start | bytes 12292
  0.0 8.6 %copy-start.1 = (s32[4,256]{1,0:T(4,128)S(1)}, s32[4,256]{1,0:T(4,128)}, u32[]{:S(2)}) copy-start(s32[4,256]{1,0:T(4,128)} %exit_rows_ref.1) | copy-start | bytes 12292
  8.6 1.0 %copy-start = (f32[3,176,128]{2,1,0:T(8,128)S(1)}, f32[3,176,128]{2,1,0:T(8,128)}, u32[]{:S(2)}) copy-start(f32[3,176,128]{2,1,0:T(8,128)} %exchange.1.source_ref) | copy-start | bytes 811012

commit v2 on v1

--- a/solution.py
+++ b/solution.py
@@ -21,6 +21,7 @@
 CENTER = 0.5 * (UPPER_BOUND + LOWER_BOUND)
 LANES = 128
 SUB = 8
+UNROLL = 4
 HALO = COARSEN * CSWEEPS
 COARSE_HALO = HALO // COARSEN
 
@@ -223,7 +224,9 @@
                 body(i, pl.multiple_of(i * SUB + SUB, SUB))
                 return carry
 
-            lax.fori_loop(low, high, step, 0)
+            count = high - low
+            unroll = max(u for u in range(1, UNROLL + 1) if count % u == 0)
+            lax.fori_loop(low, high, step, 0, unroll=unroll)
 
         return run
 
@@ -261,19 +264,32 @@
     fine = jnp.where(fine < cols + LANES // 2, fine, fine - ring + COARSEN * LANES) // COARSEN
     belongs = (fine == lax.broadcasted_iota(jnp.int32, (ring, LANES), 1)).astype(jnp.float32)
 
-    def restrict(ref, offset, *lead):
-        total = None
+    belongs = belongs.astype(jnp.bfloat16)
+
+    def split(value):
+        high = value.astype(jnp.bfloat16)
+        low = (value - high.astype(jnp.float32)).astype(jnp.bfloat16)
+        return jnp.concatenate([high, low], axis=0)
+
+    def product(value, matrix, dims):
+        both = lax.dot_general(
+            split(value), matrix, (dims, ((), ())), preferred_element_type=jnp.float32
+        )
+        size = value.shape[0]
+        return both[:size] + both[size:]
+
+    def restrict(ref, offset, leads):
+        stacked = []
         for t in range(span):
-            block = ref[(*lead, t, pl.ds(offset, coarse_rows, stride=COARSEN), slice(None))]
-            for k in range(1, COARSEN):
-                block = block + ref[
-                    (*lead, t, pl.ds(offset + k, coarse_rows, stride=COARSEN), slice(None))
+            blocks = []
+            for lead in leads:
+                part = [
+                    ref[(*lead, t, pl.ds(offset + k, coarse_rows, stride=COARSEN), slice(None))]
+                    for k in range(COARSEN)
                 ]
-            part = lax.dot_general(
-                block, belongs[t * LANES : (t + 1) * LANES], (((1,), (0,)), ((), ())),
-                precision=lax.Precision.HIGHEST, preferred_element_type=jnp.float32,
-            )
-            total = part if total is None else total + part
+                blocks.append((part[0] + part[1]) + (part[2] + part[3]))
+            stacked.append(jnp.concatenate(blocks, axis=0) if len(blocks) > 1 else blocks[0])
+        total = product(jnp.concatenate(stacked, axis=1), belongs, ((1,), (0,)))
         return total * (1.0 / (COARSEN * COARSEN))
 
     shape = (coarse_rows, LANES)
@@ -291,29 +307,25 @@
     def coarse_solve(rhs):
         center_weight = 4.0 + COARSE_SHIFT
         gain = DAMPING / center_weight
-        estimate = gain * rhs * floor
+        size = rhs.shape[0]
+        inside = jnp.concatenate([floor] * (size // coarse_rows), axis=0)
+        estimate = gain * rhs * inside
         for sweep in range(CSWEEPS - 1):
             around = (
-                pltpu.roll(estimate, coarse_rows - 1, 0) + pltpu.roll(estimate, 1, 0)
+                pltpu.roll(estimate, size - 1, 0) + pltpu.roll(estimate, 1, 0)
                 + pltpu.roll(estimate, LANES - 1, 1) + pltpu.roll(estimate, 1, 1)
             )
-            estimate = ((1.0 - DAMPING) * estimate + gain * (rhs + around)) * floor
+            estimate = ((1.0 - DAMPING) * estimate + gain * (rhs + around)) * inside
         return estimate
-
-    def widen(estimate, t):
-        return lax.dot_general(
-            estimate, belongs[t * LANES : (t + 1) * LANES], (((1,), (1,)), ((), ())),
-            precision=lax.Precision.HIGHEST, preferred_element_type=jnp.float32,
-        )
 
     def spread(ref, i, t, *lead):
         even = jnp.broadcast_to(ref[(*lead, t, pl.ds(2 * i, 1), slice(None))], (SUB, LANES))
         odd = jnp.broadcast_to(ref[(*lead, t, pl.ds(2 * i + 1, 1), slice(None))], (SUB, LANES))
         return jnp.where(sub < COARSEN, even, odd)
 
-    estimate = coarse_solve(restrict(source_ref, SUB))
+    fine_columns = product(coarse_solve(restrict(source_ref, SUB, [()])), belongs, ((1,), (1,)))
     for t in range(span):
-        expand_ref[t] = widen(estimate, t)
+        expand_ref[t] = fine_columns[:, t * LANES : (t + 1) * LANES]
 
     @loop(0, groups)
     def _(i, at):
@@ -365,10 +377,13 @@
                     residual + kept * correction[t] + opened[t] * around_corr[t]
                 )
 
+    estimates = coarse_solve(restrict(rest_ref, 0, [(g,) for g in range(goals)]))
+    fine_columns = product(estimates, belongs[:cols], ((1,), (1,)))
     for g in range(goals):
-        estimate = coarse_solve(restrict(rest_ref, 0, g))
         for t in range(tiles):
-            last_ref[g, t] = widen(estimate, t)
+            last_ref[g, t] = fine_columns[
+                g * coarse_rows : (g + 1) * coarse_rows, t * LANES : (t + 1) * LANES
+            ]
 
     edge = HALO // SUB
 

time: 28.9 us -> 18.1 us (0.63)
  Pallas kernels: 27.8 us -> 17 us
    pallas_call x1, Pallas kernels: 19.2 us -> 8.44 us  [per_device(): pl.pallas_call(functools.partial(cycles_kernel, peers), out_shape=jax.Sha...]
where the time goes in v2:
time: 18.1 us; the launch traced here: 18 us
  Pallas kernels  17 us (94%)
  local copies, waits for them, and re-layouts  0.95 us (5%)
    pallas_call x1, Pallas kernels, per_device(): pl.pallas_call(functools.partial(exchange_kernel, peers), out_shape=jax.S...  8.54 us
    pallas_call x1, Pallas kernels, per_device(): pl.pallas_call(functools.partial(cycles_kernel, peers), out_shape=jax.Sha...  8.44 us
    unnamed x6, local copies, waits for them, and re-layouts  0.95 us

profile of v2, /device:TPU:0, one launch (start us, length us, event | category | flops | bytes accessed | tf_op | source)
XLA Modules:
  0.0 18.0 jit_solution(13795712686427911872)
XLA Ops:
  0.0 0.0 copy-start.2
  0.0 0.0 copy-start.1
  0.0 8.5 %exchange.1.source_ref = f32[3,176,128]{2,1,0:T(8,128)} custom-call(s32[128,256]{1,0:T(8,128)} %obst_ref.1, f32[128,256]{1,0:T(8,128)} %load_ref.1), custom_call_target="tpu_custom_call" | custom-call | tf_op jit(solution)/shard_map/exchange/pallas_call | solution.py:431
  8.6 0.0 copy-done.2
  8.6 0.0 copy-done.1
  8.6 0.0 copy-start
  8.6 0.9 %copy-done = f32[3,176,128]{2,1,0:T(8,128)S(1)} copy-done((f32[3,176,128]{2,1,0:T(8,128)S(1)}, f32[3,176,128]{2,1,0:T(8,128)}, u32[]{:S(2)}) %copy-start) | copy-done | bytes 270360
  9.5 8.4 %cycles.1 = f32[4,128,256]{2,1,0:T(8,128)} custom-call(f32[3,176,128]{2,1,0:T(8,128)S(1)} %copy-done, s32[4,256]{1,0:T(4,128)S(1)} %copy-done.1, s32[4,256]{1,0:T(4,128)S(1)} %copy-done.2), custom_call_target="tpu_custom_call" | custom-call | tf_op jit(solution)/shard_map/cycles/pallas_call | solution.py:454
Async XLA Ops:
  0.0 8.6 %copy-start.2 = (s32[4,256]{1,0:T(4,128)S(1)}, s32[4,256]{1,0:T(4,128)}, u32[]{:S(2)}) copy-start(s32[4,256]{1,0:T(4,128)} %exit_cols_ref.1) | copy-start | bytes 12292
  0.0 8.6 %copy-start.1 = (s32[4,256]{1,0:T(4,128)S(1)}, s32[4,256]{1,0:T(4,128)}, u32[]{:S(2)}) copy-start(s32[4,256]{1,0:T(4,128)} %exit_rows_ref.1) | copy-start | bytes 12292
  8.6 1.0 %copy-start = (f32[3,176,128]{2,1,0:T(8,128)S(1)}, f32[3,176,128]{2,1,0:T(8,128)}, u32[]{:S(2)}) copy-start(f32[3,176,128]{2,1,0:T(8,128)} %exchange.1.source_ref) | copy-start | bytes 811012

commit v3 on v2

--- a/solution.py
+++ b/solution.py
@@ -21,7 +21,7 @@
 CENTER = 0.5 * (UPPER_BOUND + LOWER_BOUND)
 LANES = 128
 SUB = 8
-UNROLL = 4
+UNROLL = 6
 HALO = COARSEN * CSWEEPS
 COARSE_HALO = HALO // COARSEN
 
@@ -59,9 +59,9 @@
     return lax.broadcasted_iota(jnp.int32, (rows, LANES), 1)
 
 
-def exchange_kernel(
-    peers, obst_ref, load_ref, out_ref, top, bot, lef, rig, from_rows, from_cols, from_corners,
-    send_sem, recv_sem,
+def exchange(
+    peers, inputs, obst_ref, load_ref, out_ref, top, bot, lef, rig, from_rows, from_cols,
+    from_corners, send_sem, recv_sem, meanwhile,
 ):
     rows, cols = obst_ref.shape
     tiles = cols // LANES
@@ -83,6 +83,11 @@
                 barrier, inc=1, device_id=(me[0] + dx, me[1] + dy),
                 device_id_type=pl.DeviceIdType.MESH,
             )
+
+    for copied in inputs:
+        copied.start()
+    for copied in inputs:
+        copied.wait()
 
     def source(start, size, tile):
         block = (pl.ds(start, size), pl.ds(tile * LANES, LANES))
@@ -142,6 +147,8 @@
     for tile in range(tiles):
         out_ref[tile, pl.ds(first, rows), :] = source(0, rows, tile)
 
+    meanwhile()
+
     for k in order:
         dx, dy = DIRECTIONS[k]
 
@@ -181,9 +188,11 @@
 
 
 def cycles_kernel(
-    peers, source_ref, exit_rows_ref, exit_cols_ref, out_ref,
+    peers, obst_hbm, load_hbm, rows_hbm, cols_hbm, out_ref,
+    obst_ref, load_ref, exit_rows_ref, exit_cols_ref, source_ref,
     open_ref, marks_ref, diag_ref, first_ref, second_ref, rest_ref, shift_ref,
     expand_ref, corr_ref, fixed_ref, last_ref,
+    top, bot, lef, rig, from_rows, from_cols, from_corners, input_sem, send_sem, recv_sem,
 ):
     goals, rows, cols = out_ref.shape
     tiles = cols // LANES
@@ -230,14 +239,41 @@
 
         return run
 
-    zero = jnp.zeros((SUB, LANES), jnp.float32)
-    for ends in (0, wide + SUB):
-        for t in range(span):
-            open_ref[t, pl.ds(ends, SUB), :] = zero
-            corr_ref[t, pl.ds(ends, SUB), :] = zero
-            for g in range(goals):
-                for ref in (first_ref, second_ref):
-                    ref[g, t, pl.ds(ends, SUB), :] = zero
+    def meanwhile():
+        zero = jnp.zeros((SUB, LANES), jnp.float32)
+        for ends in (0, wide + SUB):
+            for t in range(span):
+                open_ref[t, pl.ds(ends, SUB), :] = zero
+                corr_ref[t, pl.ds(ends, SUB), :] = zero
+                for g in range(goals):
+                    for ref in (first_ref, second_ref):
+                        ref[g, t, pl.ds(ends, SUB), :] = zero
+
+        count = exit_rows_ref.shape[1]
+        row_of = lax.broadcasted_iota(jnp.int32, (wide, count), 0) + (row_start - HALO)
+        ring_lane = lax.broadcasted_iota(jnp.int32, (ring, count), 0)
+        col_of = jnp.where(ring_lane < cols + LANES // 2, ring_lane, ring_lane - ring) + col_start
+        for g in range(goals):
+            row_hot = (row_of == exit_rows_ref[pl.ds(g, 1), :]).astype(jnp.float32)
+            col_hot = (col_of == exit_cols_ref[pl.ds(g, 1), :]).astype(jnp.float32)
+            marks = lax.dot_general(
+                row_hot.astype(jnp.bfloat16), col_hot.astype(jnp.bfloat16),
+                (((1,), (1,)), ((), ())), preferred_element_type=jnp.float32,
+            )
+            for t in range(span):
+                marks_ref[g, t] = marks[:, t * LANES : (t + 1) * LANES]
+
+    pairs = (
+        (obst_hbm, obst_ref), (load_hbm, load_ref), (rows_hbm, exit_rows_ref),
+        (cols_hbm, exit_cols_ref),
+    )
+    inputs = [
+        pltpu.make_async_copy(there, here, input_sem.at[k]) for k, (there, here) in enumerate(pairs)
+    ]
+    exchange(
+        peers, inputs, obst_ref, load_ref, source_ref, top, bot, lef, rig, from_rows, from_cols,
+        from_corners, send_sem, recv_sem, meanwhile,
+    )
 
     @loop(0, groups)
     def _(i, at):
@@ -245,20 +281,6 @@
             open_ref[t, pl.ds(at, SUB), :] = (source_ref[t, pl.ds(at, SUB), :] > 0.0).astype(
                 jnp.float32
             )
-
-    count = exit_rows_ref.shape[1]
-    row_of = lax.broadcasted_iota(jnp.int32, (wide, count), 0) + (row_start - HALO)
-    ring_lane = lax.broadcasted_iota(jnp.int32, (ring, count), 0)
-    col_of = jnp.where(ring_lane < cols + LANES // 2, ring_lane, ring_lane - ring) + col_start
-    for g in range(goals):
-        row_hot = (row_of == exit_rows_ref[pl.ds(g, 1), :]).astype(jnp.float32)
-        col_hot = (col_of == exit_cols_ref[pl.ds(g, 1), :]).astype(jnp.float32)
-        marks = lax.dot_general(
-            row_hot.astype(jnp.bfloat16), col_hot.astype(jnp.bfloat16),
-            (((1,), (1,)), ((), ())), preferred_element_type=jnp.float32,
-        )
-        for t in range(span):
-            marks_ref[g, t] = marks[:, t * LANES : (t + 1) * LANES]
 
     fine = lax.broadcasted_iota(jnp.int32, (ring, LANES), 0)
     fine = jnp.where(fine < cols + LANES // 2, fine, fine - ring + COARSEN * LANES) // COARSEN
@@ -428,12 +450,25 @@
     f32 = jnp.float32
     vmem = pl.BlockSpec(memory_space=pltpu.VMEM)
     packed = rows * HALO // LANES
-    source = pl.pallas_call(
-        functools.partial(exchange_kernel, peers),
-        out_shape=jax.ShapeDtypeStruct((span, padded, LANES), f32),
-        in_specs=[vmem] * 2,
+    exits = exit_rows.shape
+    field = pltpu.VMEM((goals, span, padded, LANES), f32)
+    flat = pltpu.VMEM((goals, span, wide, LANES), f32)
+    shared = pltpu.VMEM((span, padded, LANES), f32)
+    coarse = wide // COARSEN
+    return pl.pallas_call(
+        functools.partial(cycles_kernel, peers),
+        out_shape=jax.ShapeDtypeStruct((goals, rows, cols), f32),
+        in_specs=[pl.BlockSpec(memory_space=pltpu.HBM)] * 4,
         out_specs=vmem,
         scratch_shapes=[
+            pltpu.VMEM((rows, cols), jnp.int32),
+            pltpu.VMEM((rows, cols), f32),
+            pltpu.VMEM(exits, jnp.int32),
+            pltpu.VMEM(exits, jnp.int32),
+            shared,
+            shared, flat, field, field, field, flat, field,
+            pltpu.VMEM((span, coarse, LANES), f32), shared, field,
+            pltpu.VMEM((goals, tiles, coarse, LANES), f32),
             pltpu.VMEM((tiles, HALO, LANES), f32),
             pltpu.VMEM((tiles, HALO, LANES), f32),
             pltpu.VMEM((packed, LANES), f32),
@@ -441,29 +476,15 @@
             pltpu.VMEM((2, tiles, HALO, LANES), f32),
             pltpu.VMEM((2, packed, LANES), f32),
             pltpu.VMEM((4, HALO, LANES), f32),
+            pltpu.SemaphoreType.DMA((4,)),
             pltpu.SemaphoreType.DMA((len(DIRECTIONS),)),
             pltpu.SemaphoreType.DMA((len(DIRECTIONS),)),
         ],
-        compiler_params=pltpu.CompilerParams(collective_id=0, has_side_effects=True),
-        name="exchange",
-    )(obstacles, load)
-    field = pltpu.VMEM((goals, span, padded, LANES), f32)
-    flat = pltpu.VMEM((goals, span, wide, LANES), f32)
-    shared = pltpu.VMEM((span, padded, LANES), f32)
-    coarse = wide // COARSEN
-    return pl.pallas_call(
-        functools.partial(cycles_kernel, peers),
-        out_shape=jax.ShapeDtypeStruct((goals, rows, cols), f32),
-        in_specs=[vmem] * 3,
-        out_specs=vmem,
-        scratch_shapes=[
-            shared, flat, field, field, field, flat, field,
-            pltpu.VMEM((span, coarse, LANES), f32), shared, field,
-            pltpu.VMEM((goals, tiles, coarse, LANES), f32),
-        ],
-        compiler_params=pltpu.CompilerParams(vmem_limit_bytes=48 * 1024 * 1024),
+        compiler_params=pltpu.CompilerParams(
+            collective_id=0, has_side_effects=True, vmem_limit_bytes=48 * 1024 * 1024
+        ),
         name="cycles",
-    )(source, exit_rows, exit_cols)
+    )(*(pltpu.with_memory_space_constraint(x, pltpu.HBM) for x in (obstacles, load, exit_rows, exit_cols)))
 
 
 def solution(mesh):

time: 18.1 us -> 14.5 us (0.80)
  Pallas kernels: 17 us -> 13.6 us
    pallas_call x1 -> x0, Pallas kernels: 8.54 us -> none  [per_device(): pl.pallas_call(functools.partial(exchange_kernel, peers), out_shape=jax.S...]
    pallas_call x1, Pallas kernels: 8.44 us -> 13.6 us  [per_device(): pl.pallas_call(functools.partial(cycles_kernel, peers), out_shape=jax.Sha...]
    unnamed x6 -> x1, local copies, waits for them, and re-layouts: 0.95 us -> 0.8 us
where the time goes in v3:
time: 14.5 us; the launch traced here: 14.4 us
  Pallas kernels  13.6 us (94%)
  local copies, waits for them, and re-layouts  0.8 us (6%)
    pallas_call x1, Pallas kernels, per_device(): pl.pallas_call(functools.partial(cycles_kernel, peers), out_shape=jax.Sha...  13.6 us
    unnamed x1, local copies, waits for them, and re-layouts  0.8 us

profile of v3, /device:TPU:0, one launch (start us, length us, event | category | flops | bytes accessed | tf_op | source)
XLA Modules:
  0.0 14.4 jit_solution(8231298010769967223)
XLA Ops:
  0.0 13.6 %cycles.1 = f32[4,128,256]{2,1,0:T(8,128)S(1)} custom-call(s32[128,256]{1,0:T(8,128)} %obst_hbm.1, f32[128,256]{1,0:T(8,128)} %load_hbm.1, s32[4,256]{1,0:T(4,128)} %rows_hbm.1, s32[4,256]{1,0:T(4,128)} %cols_hbm.1), custom_call_target="tpu_custom_call" | custom-call | tf_op jit(solution)/shard_map/cycles/pallas_call | solution.py:458
  13.6 0.8 %copy.6 = f32[4,128,256]{2,1,0:T(8,128)} copy(f32[4,128,256]{2,1,0:T(8,128)S(1)} %cycles.1) | data formatting | bytes 1048576

commit v4 on v3

--- a/solution.py
+++ b/solution.py
@@ -21,7 +21,7 @@
 CENTER = 0.5 * (UPPER_BOUND + LOWER_BOUND)
 LANES = 128
 SUB = 8
-UNROLL = 6
+UNROLL = 10
 HALO = COARSEN * CSWEEPS
 COARSE_HALO = HALO // COARSEN
 

time: 14.5 us -> 13.6 us (0.938)
  Pallas kernels: 13.6 us -> 12.7 us
    pallas_call x1, Pallas kernels: 13.6 us -> 12.7 us  [per_device(): pl.pallas_call(functools.partial(cycles_kernel, peers), out_shape=jax.Sha...]
where the time goes in v4:
time: 13.6 us; the launch traced here: 13.5 us
  Pallas kernels  12.7 us (93%)
  local copies, waits for them, and re-layouts  0.8 us (6%)
    pallas_call x1, Pallas kernels, per_device(): pl.pallas_call(functools.partial(cycles_kernel, peers), out_shape=jax.Sha...  12.7 us
    unnamed x1, local copies, waits for them, and re-layouts  0.8 us

profile of v4, /device:TPU:0, one launch (start us, length us, event | category | flops | bytes accessed | tf_op | source)
XLA Modules:
  0.0 13.5 jit_solution(15527874973679877886)
XLA Ops:
  0.0 12.7 %cycles.1 = f32[4,128,256]{2,1,0:T(8,128)S(1)} custom-call(s32[128,256]{1,0:T(8,128)} %obst_hbm.1, f32[128,256]{1,0:T(8,128)} %load_hbm.1, s32[4,256]{1,0:T(4,128)} %rows_hbm.1, s32[4,256]{1,0:T(4,128)} %cols_hbm.1), custom_call_target="tpu_custom_call" | custom-call | tf_op jit(solution)/shard_map/cycles/pallas_call | solution.py:458
  12.7 0.8 %copy.6 = f32[4,128,256]{2,1,0:T(8,128)} copy(f32[4,128,256]{2,1,0:T(8,128)S(1)} %cycles.1) | data formatting | bytes 1048576
